TPU v7x, 32 devices: a whole 2x2x4 slice. The times are simulated.
32 devices in a mesh: slab: 4 (over z), sub: 8 (over y, x, core).
Axes of the slice: x: 2, y: 2, z: 4, core: 2. Of those that a mesh axis runs over, the one named last changes fastest.
Arguments:
- near_null: float32 [18, 16384], P(None, ('slab', 'sub')), may hold values from -48 to 48
- aggregates: int32 [16384], P(('slab', 'sub')), may hold values from 0 to 63
- diag_block: float32 [9, 16384], P(None, ('slab', 'sub')), may hold values from -1 to 12, as said below
- off_blocks: float32 [26, 9, 16384], P(None, None, ('slab', 'sub')), may hold values from -18 to 18
- columns: int32 [26, 16384], P(None, ('slab', 'sub')), may hold values from 0 to 767, as said below
- sends: int32 [4, 2048], P(None, ('slab', 'sub')), may hold values from 0 to 511
- start_vector: float32 [3, 16384], P(None, ('slab', 'sub')), may hold values from -18 to 18
Outputs:
- prolong_off: bfloat16 [26, 18, 16384], P(None, None, ('slab', 'sub'))
- prolong_self: bfloat16 [18, 16384], P(None, ('slab', 'sub'))
- rho: float32 [], replicated
Inputs may be any that keep to these rules, and one draw needn't show every extreme that they name: `diag_block`: each block, read as 3x3 row-major, is symmetric with diagonal entries between 6 and 12 and off-diagonal entries between -1 and 1. `columns`: entries below 512 name a node of the same device; an entry c of 512 or more names ghost slot c - 512. Row e lists, for each device, the local rows it sends to its neighbour at sub + 1, sub - 1, slab + 1, slab - 1 for e = 0, 1, 2, 3. `aggregates`: aggregates lie within one device.
All inputs are finite; a program needn't handle non-finite values.
Results may differ from a plain program's by a relative error of at most 0.001.
Values sent between devices are 32-bit elements; how exact they have to be, the bound alone decides.
A program may use at most 64 MiB of HBM per device.

v0:
```python
import functools

import jax
import jax.numpy as jnp
from jax import lax
from jax.experimental import pallas as pl
from jax.experimental.pallas import tpu as pltpu
from jax.sharding import PartitionSpec as P

ITERS = 8
OMEGA = 4.0 / 3.0
LANES = 128
MESH = pl.DeviceIdType.MESH


def lane_gather(table, lanes):
    return jnp.take_along_axis(table, lanes, axis=1, mode="promise_in_bounds")


def tile(number):
    return pl.ds(number * LANES, LANES)


def pick(tables, index, first):
    high = index >> 7
    low = index & (LANES - 1)
    out = jnp.zeros(index.shape, jnp.float32)
    for step, table in enumerate(tables):
        out = jnp.where(high == first + step, lane_gather(table, low), out)
    return out


def invert_rows(entries):
    cofactor = [
        entries[4] * entries[8] - entries[5] * entries[7],
        entries[5] * entries[6] - entries[3] * entries[8],
        entries[3] * entries[7] - entries[4] * entries[6],
        entries[2] * entries[7] - entries[1] * entries[8],
        entries[0] * entries[8] - entries[2] * entries[6],
        entries[1] * entries[6] - entries[0] * entries[7],
        entries[1] * entries[5] - entries[2] * entries[4],
        entries[2] * entries[3] - entries[0] * entries[5],
        entries[0] * entries[4] - entries[1] * entries[3],
    ]
    determinant = entries[0] * cofactor[0] + entries[1] * cofactor[1] + entries[2] * cofactor[2]
    return [
        cofactor[column * 3 + row] / determinant for row in range(3) for column in range(3)
    ]


def kernel(
    n_slab, n_sub,
    near_ref, agg_ref, diag_ref, off_hbm, cols_ref, sends_ref, start_ref,
    raw_ref, tent_ref, rho_ref,
    off_v, cols_p, cols_k, mats, dinv, text, hist, sidx,
    sendw, recvw, sendt, recvt, stat_a, stats_a, stat_b, stats_b,
    off_sem, sendw_sem, recvw_sem, sendt_sem, recvt_sem,
    sa_sem, ra_sem, sb_sem, rb_sem,
):
    slots, rows = cols_ref.shape
    half = sends_ref.shape[1]
    tiles = rows // LANES
    ktiles = cols_p.shape[0] // 8
    modes = near_ref.shape[0] // 3
    groups = rows // 8
    a = lax.axis_index("slab")
    b = lax.axis_index("sub")
    load = pltpu.make_async_copy(off_hbm, off_v.at[pl.ds(0, slots)], off_sem)
    load.start()

    recvw[...] = jnp.zeros_like(recvw)
    recvt[...] = jnp.zeros_like(recvt)
    barrier = pltpu.get_barrier_semaphore()
    for step in range(1, n_sub):
        pl.semaphore_signal(
            barrier, inc=1, device_id={"sub": lax.rem(b + step, n_sub)}, device_id_type=MESH
        )
    for step in range(1, n_slab):
        pl.semaphore_signal(
            barrier, inc=1, device_id={"slab": lax.rem(a + step, n_slab)}, device_id_type=MESH
        )

    ways = (
        ("sub", b + 1, 0, b < n_sub - 1, b > 0),
        ("sub", b - 1, 0, b > 0, b < n_sub - 1),
        ("slab", a + 1, 1, a < n_slab - 1, a > 0),
        ("slab", a - 1, 1, a > 0, a < n_slab - 1),
    )

    def w_copy(t, way):
        axis, target, pair, unused, unused2 = ways[way]
        return pltpu.make_async_remote_copy(
            src_ref=sendw.at[t, pair], dst_ref=recvw.at[t, way],
            send_sem=sendw_sem.at[t, way], recv_sem=recvw_sem.at[t, way],
            device_id={axis: target}, device_id_type=MESH,
        )

    def t_copy(way):
        axis, target, pair, unused, unused2 = ways[way]
        return pltpu.make_async_remote_copy(
            src_ref=sendt.at[pair], dst_ref=recvt.at[way],
            send_sem=sendt_sem.at[way], recv_sem=recvt_sem.at[way],
            device_id={axis: target}, device_id_type=MESH,
        )

    def each_target(make, act):
        for way in range(4):
            pl.when(ways[way][3])(functools.partial(act, make, way))

    def each_source(make):
        for way in range(4):
            pl.when(ways[way][4])(functools.partial(lambda way: make(way).wait_recv(), way))

    hist[...] = jnp.zeros_like(hist)
    hist[0, 0:3, :] = start_ref[...]
    for pair in range(2):
        sidx[pair] = jnp.broadcast_to(
            jnp.concatenate(
                [sends_ref[2 * pair : 2 * pair + 1, :], sends_ref[2 * pair + 1 : 2 * pair + 2, :]],
                axis=1,
            ),
            (8, LANES),
        )

    def pack_w(t):
        tables = [hist[t, :, tile(j)] for j in range(tiles)]
        for pair in range(2):
            sendw[t, pair] = pick(tables, sidx[pair], 0)

    pack_w(0)
    pl.semaphore_wait(barrier, n_sub - 1 + n_slab - 1)
    each_target(functools.partial(w_copy, 0), lambda make, way: make(way).start())

    agg = agg_ref[...]
    member = (
        jnp.broadcast_to(agg, (groups, rows)) == lax.broadcasted_iota(jnp.int32, (groups, rows), 0)
    ).astype(jnp.float32)
    counts = jnp.sum(member, axis=1, keepdims=True)
    sizes = jnp.sum(member * counts, axis=0, keepdims=True)
    tent = near_ref[...] * lax.rsqrt(sizes)
    tent_ref[...] = tent
    text[...] = jnp.zeros_like(text)
    for c in range(3):
        text[8 * c : 8 * c + modes, 0:rows] = tent_ref[modes * c : modes * (c + 1), :]
    for pair in range(2):
        for c in range(3):
            sendt[pair, 8 * c : 8 * c + 8, :] = pick(
                [text[8 * c : 8 * c + 8, tile(j)] for j in range(tiles)], sidx[pair], 0
            )
    each_target(t_copy, lambda make, way: make(way).start())

    cols_p[...] = jnp.zeros_like(cols_p)
    cols_p[0:slots, :] = cols_ref[...]
    for k in range(slots):
        cols_k[k] = cols_ref[k : k + 1, :]

    inverse = invert_rows([diag_ref[p : p + 1, :] for p in range(9)])
    for p in range(9):
        dinv[p : p + 1, :] = inverse[p]
    for k in range(slots, off_v.shape[0]):
        off_v[k] = jnp.zeros(off_v.shape[1:], jnp.float32)
    load.wait()
    for kt in range(ktiles):
        for j in range(tiles):
            block = [off_v[8 * kt : 8 * kt + 8, p, tile(j)] for p in range(9)]
            for r in range(3):
                scale = [
                    jnp.broadcast_to(dinv[3 * r + q : 3 * r + q + 1, tile(j)], (8, LANES))
                    for q in range(3)
                ]
                for c in range(3):
                    mats[3 * r + c, 8 * kt : 8 * kt + 8, tile(j)] = (
                        scale[0] * block[c] + scale[1] * block[3 + c] + scale[2] * block[6 + c]
                    )

    left = lax.broadcasted_iota(jnp.int32, (8, LANES), 1) < half
    per = -(-slots // (ITERS - 1))

    def slot_products(k, unused):
        for j in range(tiles):
            index = jnp.broadcast_to(cols_k[k, :, tile(j)], (8, LANES))
            picked = [
                pick([text[8 * c : 8 * c + 8, tile(i)] for i in range(tiles + 2)], index, 0)
                for c in range(3)
            ]

            def spread(p):
                return jnp.broadcast_to(off_v[k, p : p + 1, tile(j)], (8, LANES))

            product = [
                spread(3 * r) * picked[0]
                + spread(3 * r + 1) * picked[1]
                + spread(3 * r + 2) * picked[2]
                for r in range(3)
            ]
            for r in range(3):
                scaled = sum(
                    jnp.broadcast_to(dinv[3 * r + q : 3 * r + q + 1, tile(j)], (8, LANES))
                    * product[q]
                    for q in range(3)
                )
                raw_ref[k, modes * r : modes * (r + 1), tile(j)] = scaled[0:modes]
        return unused

    def contribute(tables, first, j, totals):
        for kt in range(ktiles):
            index = cols_p[8 * kt : 8 * kt + 8, tile(j)]
            for c in range(3):
                picked = pick(tables[c], index, first)
                for r in range(3):
                    term = mats[3 * r + c, 8 * kt : 8 * kt + 8, tile(j)] * picked
                    totals[r] = term if totals[r] is None else totals[r] + term
        return totals

    def iterate(t, unused):
        local = [
            [jnp.broadcast_to(hist[t, c : c + 1, tile(i)], (8, LANES)) for i in range(tiles)]
            for c in range(3)
        ]
        totals = [contribute(local, 0, j, [None] * 3) for j in range(tiles)]

        @pl.when(t == 1)
        def _():
            each_source(t_copy)
            for pair in range(2):
                for c in range(3):
                    text[8 * c : 8 * c + 8, tile(tiles + pair)] = jnp.where(
                        left,
                        recvt[2 * pair, 8 * c : 8 * c + 8, :],
                        recvt[2 * pair + 1, 8 * c : 8 * c + 8, :],
                    )

        lax.fori_loop(
            jnp.clip((t - 1) * per, 0, slots), jnp.clip(t * per, 0, slots), slot_products, 0
        )
        each_source(functools.partial(w_copy, t))
        merged = [jnp.where(left, recvw[t, 2 * pair], recvw[t, 2 * pair + 1]) for pair in range(2)]
        ghost = [
            [jnp.broadcast_to(merged[pair][c : c + 1], (8, LANES)) for pair in range(2)]
            for c in range(3)
        ]
        for j in range(tiles):
            total = contribute(ghost, tiles, j, totals[j])
            for r in range(3):
                hist[t + 1, r : r + 1, tile(j)] = hist[t, r : r + 1, tile(j)] + jnp.sum(
                    total[r], axis=0, keepdims=True
                )

        @pl.when(t < ITERS - 1)
        def _():
            pack_w(t + 1)
            each_target(functools.partial(w_copy, t + 1), lambda make, way: make(way).start())

        return unused

    lax.fori_loop(0, ITERS, iterate, 0)

    def squares(t):
        return jnp.sum(
            sum(hist[t, :, tile(j)] * hist[t, :, tile(j)] for j in range(tiles)),
            axis=0, keepdims=True,
        )

    row = lax.broadcasted_iota(jnp.int32, (8, LANES), 0)
    own = jnp.where(
        row == 0,
        jnp.broadcast_to(squares(ITERS), (8, LANES)),
        jnp.where(row == 1, jnp.broadcast_to(squares(ITERS - 1), (8, LANES)), 0.0),
    )

    def sum_along(value, axis, me, count, stat, stats, send_sem, recv_sem):
        stat[...] = value

        def to(step):
            return pltpu.make_async_remote_copy(
                src_ref=stat, dst_ref=stats.at[me],
                send_sem=send_sem.at[step], recv_sem=recv_sem.at[me],
                device_id={axis: lax.rem(me + step, count)}, device_id_type=MESH,
            )

        def come(step):
            source = lax.rem(me + step, count)
            return pltpu.make_async_remote_copy(
                src_ref=stat, dst_ref=stats.at[source],
                send_sem=send_sem.at[step], recv_sem=recv_sem.at[source],
                device_id={axis: source}, device_id_type=MESH,
            )

        for step in range(1, count):
            to(step).start()
        stats[me] = value
        for step in range(1, count):
            come(step).wait_recv()
        total = stats[0]
        for source in range(1, count):
            total = total + stats[source]
        for step in range(1, count):
            to(step).wait_send()
        return total

    part = sum_along(own, "sub", b, n_sub, stat_a, stats_a, sa_sem, ra_sem)
    whole = sum_along(part, "slab", a, n_slab, stat_b, stats_b, sb_sem, rb_sem)
    latest = jnp.sum(whole[0:1], axis=1, keepdims=True)
    previous = jnp.sum(whole[1:2], axis=1, keepdims=True)
    rho_ref[...] = jnp.sqrt(latest / (previous + 1e-05))

    each_target(t_copy, lambda make, way: make(way).wait_send())

    def drain(t, unused):
        each_target(functools.partial(w_copy, t), lambda make, way: make(way).wait_send())
        return unused

    lax.fori_loop(0, ITERS, drain, 0)


def body(n_slab, n_sub, near_null, aggregates, diag_block, off_blocks, columns, sends, start_vector):
    slots, nine, rows = off_blocks.shape
    padded = -(-slots // 8) * 8
    wide = rows + 2 * LANES
    f32 = jnp.float32
    vmem = pl.BlockSpec(memory_space=pltpu.VMEM)
    dma = pltpu.SemaphoreType.DMA
    raw, tentative, rho = pl.pallas_call(
        functools.partial(kernel, n_slab, n_sub),
        out_shape=(
            jax.ShapeDtypeStruct((slots, near_null.shape[0], rows), f32),
            jax.ShapeDtypeStruct(near_null.shape, f32),
            jax.ShapeDtypeStruct((1, 1), f32),
        ),
        in_specs=[vmem, vmem, vmem, pl.BlockSpec(memory_space=pl.ANY), vmem, vmem, vmem],
        out_specs=(vmem, vmem, vmem),
        scratch_shapes=[
            pltpu.VMEM((padded, nine, rows), f32),
            pltpu.VMEM((padded, rows), jnp.int32),
            pltpu.VMEM((slots, 1, rows), jnp.int32),
            pltpu.VMEM((9, padded, rows), f32),
            pltpu.VMEM((16, rows), f32),
            pltpu.VMEM((24, wide), f32),
            pltpu.VMEM((ITERS + 1, 8, rows), f32),
            pltpu.VMEM((2, 8, LANES), jnp.int32),
            pltpu.VMEM((ITERS, 2, 8, LANES), f32),
            pltpu.VMEM((ITERS, 4, 8, LANES), f32),
            pltpu.VMEM((2, 24, LANES), f32),
            pltpu.VMEM((4, 24, LANES), f32),
            pltpu.VMEM((8, LANES), f32),
            pltpu.VMEM((n_sub, 8, LANES), f32),
            pltpu.VMEM((8, LANES), f32),
            pltpu.VMEM((n_slab, 8, LANES), f32),
            dma,
            dma((ITERS, 4)),
            dma((ITERS, 4)),
            dma((4,)),
            dma((4,)),
            dma((n_sub,)),
            dma((n_sub,)),
            dma((n_slab,)),
            dma((n_slab,)),
        ],
        compiler_params=pltpu.CompilerParams(collective_id=0, has_side_effects=True),
        name="smooth",
    )(near_null, aggregates.reshape(1, rows), diag_block, off_blocks, columns, sends, start_vector)
    rho = rho.reshape(())
    factor = -(OMEGA / rho)
    prolong_off = (factor * raw).astype(jnp.bfloat16)
    prolong_self = ((1.0 - OMEGA / rho) * tentative).astype(jnp.bfloat16)
    return (prolong_off, prolong_self, rho)


def solution(mesh):
    placed = (
        P(None, ("slab", "sub")),
        P(("slab", "sub")),
        P(None, ("slab", "sub")),
        P(None, None, ("slab", "sub")),
        P(None, ("slab", "sub")),
        P(None, ("slab", "sub")),
        P(None, ("slab", "sub")),
    )
    return jax.shard_map(
        functools.partial(body, mesh.shape["slab"], mesh.shape["sub"]),
        mesh=mesh,
        in_specs=placed,
        out_specs=(P(None, None, ("slab", "sub")), P(None, ("slab", "sub")), P()),
        check_vma=False,
    )
```

profile of v0, /device:TPU:0, one launch (start us, length us, event | category | flops | bytes accessed | tf_op | source)
XLA Modules:
  0.0 47.1 jit_solution(13060642074513383024)
XLA Ops:
  0.6 2.3 %copy.10.off_hbm = f32[26,9,512]{2,1,0:T(8,128)} copy(f32[26,9,512]{2,0,1:T(8,128)} %param.10) | data formatting | bytes 958464 | tf_op args[3]
  2.9 38.5 %smooth.1 = (f32[26,18,512]{2,1,0:T(8,128)}, f32[18,512]{1,0:T(8,128)}, f32[1,1]{1,0:T(1,128)}) custom-call(f32[18,512]{1,0:T(8,128)} %near_ref.1, s32[1,512]{1,0:T(1,128)} %bitcast.2, f32[9,512]{1,0:T(8,128)} %diag_ref.1, f32[26,9,512]{2,1,0:T(8,128)} %copy.10.off_hbm, s32[26,512]{1,0:T(8,128)} %cols_ref.1, s32[4,64]{1,0:T(4,128)} %sends_ref.1, ...), custom_call_target="tpu_custom_call" | custom-call | tf_op jit(solution)/shard_map/smooth/pallas_call | solution.py:323
  42.2 0.0 copy-start
  42.2 1.5 %multiply_convert_fusion = bf16[26,18,512]{2,1,0:T(8,128)(2,1)S(1)} fusion(f32[26,18,512]{2,1,0:T(8,128)} %get-tuple-element.7, f32[]{:T(128)S(6)} %neg.3), kind=kLoop, calls=%fused_computation | loop fusion | flops 479232 | bytes 1437700 | tf_op jit(solution)/shard_map/convert_element_type | solution.py:364
  43.7 1.0 %copy.11 = bf16[26,18,512]{2,0,1:T(8,128)(2,1)} copy(bf16[26,18,512]{2,1,0:T(8,128)(2,1)S(1)} %multiply_convert_fusion) | data formatting | bytes 958464
  44.6 0.0 copy-done
  44.7 0.6 %multiply_convert_fusion.1 = bf16[18,512]{1,0:T(8,128)(2,1)} fusion(f32[18,512]{1,0:T(8,128)S(1)} %copy-done, f32[]{:T(128)S(6)} %sub.3), kind=kLoop, calls=%fused_computation.1 | loop fusion | flops 18432 | bytes 55300 | tf_op jit(solution)/shard_map/convert_element_type | solution.py:365
Async XLA Ops:
  42.2 2.5 %copy-start = (f32[18,512]{1,0:T(8,128)S(1)}, f32[18,512]{1,0:T(8,128)}, u32[]{:S(2)}) copy-start(f32[18,512]{1,0:T(8,128)} %get-tuple-element.8) | copy-start | bytes 110596
where the time goes:
time: 47.3 us; the launch traced here: 47.1 us
  Pallas kernels  38.5 us (81%)
  local copies, waits for them, and re-layouts  3.28 us (7%)
  between operations  3.18 us (7%)
  other arithmetic  2.08 us (4%)
    pallas_call x1, Pallas kernels, body(): pl.pallas_call(functools.partial(kernel, n_slab, n_sub), out_shape=(jax.S...  38.5 us
    unnamed x4, local copies, waits for them, and re-layouts  3.28 us
    convert_element_type x1, other arithmetic, body(): prolong_off = (factor * raw).astype(jnp.bfloat16)  1.47 us

commit v1 on v0

v1 whole, which is shorter than its diff:
```python
import functools

import jax
import jax.numpy as jnp
from jax import lax
from jax.experimental import pallas as pl
from jax.experimental.pallas import tpu as pltpu
from jax.sharding import PartitionSpec as P

ITERS = 8
OMEGA = 4.0 / 3.0
LANES = 128
MESH = pl.DeviceIdType.MESH


def lane_gather(table, lanes):
    return jnp.take_along_axis(table, lanes, axis=1, mode="promise_in_bounds")


def tile(number):
    return pl.ds(number * LANES, LANES)


def pick(tables, index, first):
    high = index >> 7
    low = index & (LANES - 1)
    out = jnp.zeros(index.shape, jnp.float32)
    for step, table in enumerate(tables):
        out = jnp.where(high == first + step, lane_gather(table, low), out)
    return out


def invert_rows(entries):
    cofactor = [
        entries[4] * entries[8] - entries[5] * entries[7],
        entries[5] * entries[6] - entries[3] * entries[8],
        entries[3] * entries[7] - entries[4] * entries[6],
        entries[2] * entries[7] - entries[1] * entries[8],
        entries[0] * entries[8] - entries[2] * entries[6],
        entries[1] * entries[6] - entries[0] * entries[7],
        entries[1] * entries[5] - entries[2] * entries[4],
        entries[2] * entries[3] - entries[0] * entries[5],
        entries[0] * entries[4] - entries[1] * entries[3],
    ]
    determinant = entries[0] * cofactor[0] + entries[1] * cofactor[1] + entries[2] * cofactor[2]
    return [
        cofactor[column * 3 + row] / determinant for row in range(3) for column in range(3)
    ]


def unit_places(slots, tiles):
    units = []
    for k in range(0, slots - 7, 8):
        for j in range(tiles):
            units.append([(0, k, 8, j)])
    rest = slots % 8
    if rest:
        share = 8 // rest
        for j in range(0, tiles, share):
            units.append(
                [
                    (rest * i, slots - rest, rest, j + i)
                    for i in range(min(share, tiles - j))
                ]
            )
    return units


def scale_kernel(raw_ref, tent_ref, rho_ref, off_ref, self_ref):
    slots, rows = off_ref.shape[1:]
    inverse = OMEGA / rho_ref[...]
    factor = jnp.broadcast_to(-inverse, (8, LANES))
    places = unit_places(slots, rows // LANES)
    for j in range(rows // LANES):
        for entry in range(off_ref.shape[0]):
            parts = [
                (raw_ref[entry, u] * factor)[at : at + count]
                for u in range(len(places))
                for at, k, count, tile_number in places[u]
                if tile_number == j
            ]
            off_ref[entry, :, tile(j)] = jnp.concatenate(parts, axis=0).astype(off_ref.dtype)
    self_ref[...] = ((1.0 - inverse) * tent_ref[...]).astype(self_ref.dtype)


def kernel(
    n_slab, n_sub,
    near_hbm, agg_hbm, diag_hbm, off_hbm, cols_hbm, sends_hbm, start_hbm,
    raw_hbm, tent_ref, rho_ref,
    near_ref, agg_ref, diag_ref, cols_ref, sends_ref, start_ref, raw_ref, off_v, cols_u, mats, dinv, text, hist, sidx,
    sendw, recvw, sendt, recvt, stat, stats,
    off_sem, raw_sem, sendw_sem, recvw_sem, sendt_sem, recvt_sem,
    ss_sem, rs_sem,
):
    slots, rows = cols_ref.shape
    half = sends_ref.shape[1]
    tiles = rows // LANES
    units = unit_places(slots, tiles)
    modes = near_ref.shape[0] // 3
    groups = rows // 8
    a = lax.axis_index("slab")
    b = lax.axis_index("sub")
    loads = [
        pltpu.make_async_copy(source, target, off_sem.at[number])
        for number, (source, target) in enumerate(
            (
                (start_hbm, start_ref),
                (sends_hbm, sends_ref),
                (agg_hbm, agg_ref),
                (near_hbm, near_ref),
                (diag_hbm, diag_ref),
                (cols_hbm, cols_ref),
                (off_hbm, off_v),
            )
        )
    ]
    for load in loads:
        load.start()

    recvw[...] = jnp.zeros_like(recvw)
    recvt[...] = jnp.zeros_like(recvt)
    barrier = pltpu.get_barrier_semaphore()

    def greet(step, unused):
        target = lax.rem(a * n_sub + b + step, n_slab * n_sub)
        pl.semaphore_signal(
            barrier, inc=1,
            device_id={"slab": lax.div(target, n_sub), "sub": lax.rem(target, n_sub)},
            device_id_type=MESH,
        )
        return unused

    lax.fori_loop(1, n_slab * n_sub, greet, 0)

    ways = (
        ("sub", b + 1, 0, b < n_sub - 1, b > 0),
        ("sub", b - 1, 0, b > 0, b < n_sub - 1),
        ("slab", a + 1, 1, a < n_slab - 1, a > 0),
        ("slab", a - 1, 1, a > 0, a < n_slab - 1),
    )

    def w_copy(t, way):
        axis, target, pair, unused, unused2 = ways[way]
        return pltpu.make_async_remote_copy(
            src_ref=sendw.at[t, pair], dst_ref=recvw.at[t, way],
            send_sem=sendw_sem.at[t, way], recv_sem=recvw_sem.at[t, way],
            device_id={axis: target}, device_id_type=MESH,
        )

    def t_copy(way):
        axis, target, pair, unused, unused2 = ways[way]
        return pltpu.make_async_remote_copy(
            src_ref=sendt.at[pair], dst_ref=recvt.at[way],
            send_sem=sendt_sem.at[way], recv_sem=recvt_sem.at[way],
            device_id={axis: target}, device_id_type=MESH,
        )

    def each_target(make, act):
        for way in range(4):
            pl.when(ways[way][3])(functools.partial(act, make, way))

    def each_source(make):
        for way in range(4):
            pl.when(ways[way][4])(functools.partial(lambda way: make(way).wait_recv(), way))

    hist[...] = jnp.zeros_like(hist)
    loads[0].wait()
    loads[1].wait()
    hist[0, 0:3, :] = start_ref[...]
    for pair in range(2):
        sidx[pair] = jnp.broadcast_to(
            jnp.concatenate(
                [sends_ref[2 * pair : 2 * pair + 1, :], sends_ref[2 * pair + 1 : 2 * pair + 2, :]],
                axis=1,
            ),
            (8, LANES),
        )

    def pack_w(t):
        tables = [hist[t, :, tile(j)] for j in range(tiles)]
        for pair in range(2):
            sendw[t, pair] = pick(tables, sidx[pair], 0)[0:4]

    pack_w(0)

    loads[2].wait()
    loads[3].wait()
    agg = agg_ref[...]
    member = (
        jnp.broadcast_to(agg, (groups, rows)) == lax.broadcasted_iota(jnp.int32, (groups, rows), 0)
    ).astype(jnp.float32)
    counts = jnp.sum(member, axis=1, keepdims=True)
    sizes = jnp.sum(member * counts, axis=0, keepdims=True)
    tent = near_ref[...] * lax.rsqrt(sizes)
    tent_ref[...] = tent
    text[...] = jnp.zeros_like(text)
    for c in range(3):
        text[8 * c : 8 * c + modes, 0:rows] = tent_ref[modes * c : modes * (c + 1), :]
    for pair in range(2):
        for c in range(3):
            sendt[pair, 8 * c : 8 * c + 8, :] = pick(
                [text[8 * c : 8 * c + 8, tile(j)] for j in range(tiles)], sidx[pair], 0
            )

    loads[4].wait()
    loads[5].wait()
    for u, places in enumerate(units):
        if len(places) * places[0][2] < 8:
            cols_u[u] = jnp.zeros((8, LANES), jnp.int32)
        for at, k, count, j in places:
            cols_u[u, at : at + count, :] = cols_ref[k : k + count, tile(j)]

    inverse = invert_rows([diag_ref[p : p + 1, :] for p in range(9)])
    for p in range(9):
        dinv[p : p + 1, :] = inverse[p]
    pl.semaphore_wait(barrier, n_slab * n_sub - 1)
    each_target(functools.partial(w_copy, 0), lambda make, way: make(way).start())
    each_target(t_copy, lambda make, way: make(way).start())
    loads[6].wait()
    for u, places in enumerate(units):
        if len(places) * places[0][2] < 8:
            mats[u] = jnp.zeros(mats.shape[1:], jnp.float32)
        for at, k, count, j in places:
            block = [off_v[p, k : k + count, tile(j)] for p in range(9)]
            for r in range(3):
                scale = [
                    jnp.broadcast_to(dinv[3 * r + q : 3 * r + q + 1, tile(j)], (count, LANES))
                    for q in range(3)
                ]
                for c in range(3):
                    mats[u, 3 * r + c, at : at + count, :] = (
                        scale[0] * block[c] + scale[1] * block[3 + c] + scale[2] * block[6 + c]
                    )

    left = lax.broadcasted_iota(jnp.int32, (8, LANES), 1) < half
    per = -(-len(units) // (ITERS - 1))

    def unit_products(u, unused):
        index = cols_u[u]
        for m in range(modes):
            picked = [
                pick(
                    [
                        jnp.broadcast_to(text[8 * c + m : 8 * c + m + 1, tile(i)], (8, LANES))
                        for i in range(tiles + 2)
                    ],
                    index,
                    0,
                )
                for c in range(3)
            ]
            for r in range(3):
                raw_ref[modes * r + m, u] = (
                    mats[u, 3 * r] * picked[0]
                    + mats[u, 3 * r + 1] * picked[1]
                    + mats[u, 3 * r + 2] * picked[2]
                )
        return unused

    def contribute(tables, first, u):
        index = cols_u[u]
        picked = [pick(tables[c], index, first) for c in range(3)]
        return [sum(mats[u, 3 * r + c] * picked[c] for c in range(3)) for r in range(3)]

    def by_tile(terms):
        whole = [[None] * tiles for r in range(3)]
        for r in range(3):
            for u, places in enumerate(units):
                if len(places) == 1 and places[0][2] == 8:
                    j = places[0][3]
                    old = whole[r][j]
                    whole[r][j] = terms[u][r] if old is None else old + terms[u][r]
            for j in range(tiles):
                old = whole[r][j]
                whole[r][j] = 0.0 if old is None else jnp.sum(old, axis=0, keepdims=True)
            for u, places in enumerate(units):
                if not (len(places) == 1 and places[0][2] == 8):
                    for at, k, count, j in places:
                        whole[r][j] = whole[r][j] + jnp.sum(
                            terms[u][r][at : at + count], axis=0, keepdims=True
                        )
        return whole

    def iterate(t, unused):
        local = [
            [jnp.broadcast_to(hist[t, c : c + 1, tile(i)], (8, LANES)) for i in range(tiles)]
            for c in range(3)
        ]
        inner = by_tile([contribute(local, 0, u) for u in range(len(units))])
        for r in range(3):
            for j in range(tiles):
                hist[t + 1, r : r + 1, tile(j)] = hist[t, r : r + 1, tile(j)] + inner[r][j]

        @pl.when(t == 1)
        def _():
            each_source(t_copy)
            for pair in range(2):
                for c in range(3):
                    text[8 * c : 8 * c + 8, tile(tiles + pair)] = jnp.where(
                        left,
                        recvt[2 * pair, 8 * c : 8 * c + 8, :],
                        recvt[2 * pair + 1, 8 * c : 8 * c + 8, :],
                    )

        lax.fori_loop(
            jnp.clip((t - 1) * per, 0, len(units)), jnp.clip(t * per, 0, len(units)), unit_products, 0
        )
        each_source(functools.partial(w_copy, t))
        merged = [jnp.where(left[0:4], recvw[t, 2 * pair], recvw[t, 2 * pair + 1]) for pair in range(2)]
        ghost = [
            [jnp.broadcast_to(merged[pair][c : c + 1], (8, LANES)) for pair in range(2)]
            for c in range(3)
        ]
        outer = by_tile([contribute(ghost, tiles, u) for u in range(len(units))])
        for r in range(3):
            for j in range(tiles):
                hist[t + 1, r : r + 1, tile(j)] = hist[t + 1, r : r + 1, tile(j)] + outer[r][j]

        @pl.when(t < ITERS - 1)
        def _():
            pack_w(t + 1)
            each_target(functools.partial(w_copy, t + 1), lambda make, way: make(way).start())

        return unused

    lax.fori_loop(0, ITERS, iterate, 0)

    store = pltpu.make_async_copy(raw_ref, raw_hbm, raw_sem)
    store.start()

    def squares(t):
        return jnp.sum(
            sum(hist[t, :, tile(j)] * hist[t, :, tile(j)] for j in range(tiles)), keepdims=True
        )

    lane = lax.broadcasted_iota(jnp.int32, (1, LANES), 1)
    latest = jnp.broadcast_to(squares(ITERS), (1, LANES))
    previous = jnp.broadcast_to(squares(ITERS - 1), (1, LANES))
    own = jnp.where(lane == 0, latest, jnp.where(lane == 1, previous, 0.0))
    me = a * n_sub + b
    devices = n_slab * n_sub
    stat[0] = own

    def stat_copy(step, source):
        target = lax.rem(me + step, devices)
        landing = lax.rem(me + devices - step, devices) if source else me
        return pltpu.make_async_remote_copy(
            src_ref=stat.at[0], dst_ref=stats.at[landing],
            send_sem=ss_sem.at[step], recv_sem=rs_sem.at[landing],
            device_id={"slab": lax.div(target, n_sub), "sub": lax.rem(target, n_sub)},
            device_id_type=MESH,
        )

    def begin(step, unused):
        stat_copy(step, False).start()
        return unused

    def arrive(step, unused):
        stat_copy(step, True).wait_recv()
        return unused

    def sent(step, unused):
        stat_copy(step, False).wait_send()
        return unused

    lax.fori_loop(1, devices, begin, 0)
    stats[me] = own
    lax.fori_loop(1, devices, arrive, 0)
    whole = jnp.sum(stats[...], axis=0)
    latest = whole[:, 0:1]
    previous = whole[:, 1:2]
    rho_ref[...] = jnp.sqrt(latest / (previous + 1e-05))

    lax.fori_loop(1, devices, sent, 0)
    store.wait()
    each_target(t_copy, lambda make, way: make(way).wait_send())

    def drain(t, unused):
        each_target(functools.partial(w_copy, t), lambda make, way: make(way).wait_send())
        return unused

    lax.fori_loop(0, ITERS, drain, 0)


def body(n_slab, n_sub, near_null, aggregates, diag_block, off_blocks, columns, sends, start_vector):
    slots, nine, rows = off_blocks.shape
    wide = rows + 2 * LANES
    count = len(unit_places(slots, rows // LANES))
    f32 = jnp.float32
    vmem = pl.BlockSpec(memory_space=pltpu.VMEM)
    dma = pltpu.SemaphoreType.DMA
    raw, tentative, rho = pl.pallas_call(
        functools.partial(kernel, n_slab, n_sub),
        out_shape=(
            jax.ShapeDtypeStruct((near_null.shape[0], count, 8, LANES), f32),
            jax.ShapeDtypeStruct(near_null.shape, f32),
            jax.ShapeDtypeStruct((1, 1), f32),
        ),
        in_specs=[pl.BlockSpec(memory_space=pl.ANY)] * 7,
        out_specs=(pl.BlockSpec(memory_space=pl.ANY), vmem, vmem),
        scratch_shapes=[
            pltpu.VMEM(near_null.shape, f32),
            pltpu.VMEM((1, rows), jnp.int32),
            pltpu.VMEM(diag_block.shape, f32),
            pltpu.VMEM(columns.shape, jnp.int32),
            pltpu.VMEM(sends.shape, jnp.int32),
            pltpu.VMEM(start_vector.shape, f32),
            pltpu.VMEM((near_null.shape[0], count, 8, LANES), f32),
            pltpu.VMEM((nine, slots, rows), f32),
            pltpu.VMEM((count, 8, LANES), jnp.int32),
            pltpu.VMEM((count, nine, 8, LANES), f32),
            pltpu.VMEM((16, rows), f32),
            pltpu.VMEM((24, wide), f32),
            pltpu.VMEM((ITERS + 1, 8, rows), f32),
            pltpu.VMEM((2, 8, LANES), jnp.int32),
            pltpu.VMEM((ITERS, 2, 4, LANES), f32),
            pltpu.VMEM((ITERS, 4, 4, LANES), f32),
            pltpu.VMEM((2, 24, LANES), f32),
            pltpu.VMEM((4, 24, LANES), f32),
            pltpu.VMEM((1, 1, LANES), f32),
            pltpu.VMEM((n_slab * n_sub, 1, LANES), f32),
            dma((7,)),
            dma,
            dma((ITERS, 4)),
            dma((ITERS, 4)),
            dma((4,)),
            dma((4,)),
            dma((n_slab * n_sub,)),
            dma((n_slab * n_sub,)),
        ],
        compiler_params=pltpu.CompilerParams(collective_id=0, has_side_effects=True),
        name="smooth",
    )(
        near_null, aggregates.reshape(1, rows), diag_block, off_blocks.transpose(1, 0, 2),
        columns, sends, start_vector,
    )
    prolong_off, prolong_self = pl.pallas_call(
        scale_kernel,
        out_shape=(
            jax.ShapeDtypeStruct((near_null.shape[0], slots, rows), jnp.bfloat16),
            jax.ShapeDtypeStruct(near_null.shape, jnp.bfloat16),
        ),
        in_specs=[vmem, vmem, vmem],
        out_specs=(vmem, vmem),
        name="scale",
    )(raw, tentative, rho)
    return (prolong_off.transpose(1, 0, 2), prolong_self, rho.reshape(()))


def solution(mesh):
    placed = (
        P(None, ("slab", "sub")),
        P(("slab", "sub")),
        P(None, ("slab", "sub")),
        P(None, None, ("slab", "sub")),
        P(None, ("slab", "sub")),
        P(None, ("slab", "sub")),
        P(None, ("slab", "sub")),
    )
    return jax.shard_map(
        functools.partial(body, mesh.shape["slab"], mesh.shape["sub"]),
        mesh=mesh,
        in_specs=placed,
        out_specs=(P(None, None, ("slab", "sub")), P(None, ("slab", "sub")), P()),
        check_vma=False,
    )
```

time: 47.3 us -> 41.6 us (0.88)
  local copies, waits for them, and re-layouts: 3.28 us -> 0 us
  other arithmetic: 2.08 us -> 0 us
  between operations: 3.18 us -> 2.46 us
    unnamed x4 -> x0, local copies, waits for them, and re-layouts: 3.28 us -> none
    pallas_call x0 -> x1, Pallas kernels: none -> 2.87 us  [body(): pl.pallas_call(scale_kernel, out_shape=(jax.ShapeDtypeStruct((near_null.s...]
    pallas_call x1, Pallas kernels: 38.5 us -> 36 us  [body(): pl.pallas_call(functools.partial(kernel, n_slab, n_sub), out_shape=(jax.S...]
    convert_element_type x2 -> x0, other arithmetic: 2.08 us -> none  [the longest x1 1.47 us: body(): prolong_off = (factor * raw).astype(jnp.bfloat16)]
where the time goes in v1:
time: 41.6 us; the launch traced here: 41.4 us
  Pallas kernels  38.9 us (94%)
  between operations  2.46 us (6%)
    pallas_call x1, Pallas kernels, body(): pl.pallas_call(functools.partial(kernel, n_slab, n_sub), out_shape=(jax.S...  36 us
    pallas_call x1, Pallas kernels, body(): pl.pallas_call(scale_kernel, out_shape=(jax.ShapeDtypeStruct((near_null.s...  2.87 us

profile of v1, /device:TPU:0, one launch (start us, length us, event | category | flops | bytes accessed | tf_op | source)
XLA Modules:
  0.0 41.4 jit_solution(15429062600698483015)
XLA Ops:
  0.6 36.0 %smooth.1 = (f32[18,13,8,128]{3,2,1,0:T(8,128)}, f32[18,512]{1,0:T(8,128)}, f32[1,1]{1,0:T(1,128)}) custom-call(f32[18,512]{1,0:T(8,128)} %near_hbm.1, s32[1,512]{1,0:T(1,128)} %bitcast.5, f32[9,512]{1,0:T(8,128)} %diag_hbm.1, f32[9,26,512]{2,1,0:T(8,128)} %bitcast.4, s32[26,512]{1,0:T(8,128)} %cols_hbm.1, s32[4,64]{1,0:T(4,128)} %sends_hbm.1, ...), custom_call_target="tpu_custom_call" | custom-call | tf_op jit(solution)/shard_map/smooth/pallas_call | solution.py:392
  36.7 2.9 %scale.1 = (bf16[18,26,512]{2,1,0:T(8,128)(2,1)}, bf16[18,512]{1,0:T(8,128)(2,1)}) custom-call(f32[18,13,8,128]{3,2,1,0:T(8,128)} %get-tuple-element.8.raw_ref, f32[18,512]{1,0:T(8,128)} %get-tuple-element.9.tent_ref, f32[1,1]{1,0:T(1,128)} %get-tuple-element.10.rho_ref), custom_call_target="tpu_custom_call" | custom-call | tf_op jit(solution)/shard_map/scale/pallas_call | solution.py:437
